TPU v7x, 32 devices: a whole 2x2x4 slice. The times are simulated.
32 devices in a mesh: inner: 4 (over z), outer: 8 (over y, x, core).
Axes of the slice: x: 2, y: 2, z: 4, core: 2. Of those that a mesh axis runs over, the one named last changes fastest.
Arguments:
- inner_state: float32 [2, 16, 2048], P(None, 'inner', 'outer'), may hold values from -6 to 6
- outer_state: float32 [2, 640, 4096], P(None, 'inner', 'outer'), may hold values from -6 to 6
- energies: float32 [16, 2048], P('inner', 'outer'), may hold values from -2 to 2
- dipole: float32 [16, 2048, 2048], P('inner', 'outer'), may hold values from -0.125 to 0.125
- surface: float32 [16, 40, 2048], P('inner', None, 'outer'), may hold values from -0.125 to 0.125
- thresholds: float32 [640], P('inner'), may hold values from 0 to 2
- coupling_coef: float32 [16, 40, 40], P('inner'), may hold values from -1 to 1
- coupling_pattern: int32 [16, 40, 40], P('inner'), may hold values 0 or 1
- block_sizes: int32 [16], P('inner'), may hold values from 1 to 2048, 30720 in all
- field_strength: float32 [2], replicated, may hold values from 0.5 to 2
Outputs:
- inner_final: float32 [2, 16, 2048], P(None, 'inner', 'outer')
- outer_final: float32 [2, 640, 4096], P(None, 'inner', 'outer')
All inputs are finite; a program needn't handle non-finite values. No bound on the sum of `coupling_pattern` or of `block_sizes` on one device may be relied on, other than what follows from the above.
Results may differ from a plain program's by a relative error of at most 0.0001.
Values sent between devices are 32-bit elements; how exact they have to be, the bound alone decides.
A program may use at most 128 MiB of HBM per device.

v0:
```python
import functools

import jax
import jax.numpy as jnp
from jax import lax
from jax.experimental import pallas as pl
from jax.experimental.pallas import tpu as pltpu
from jax.sharding import PartitionSpec as P

STEPS = 2
ORDER = 4

kinetic_scale = 3.125
time_step = 0.1

MESH = pl.DeviceIdType.MESH
f32 = jnp.float32
bf16 = jnp.bfloat16
NT = (((1,), (1,)), ((), ()))
NN = (((1,), (0,)), ((), ()))


def split(x):
    high = x.astype(bf16)
    return high, (x - high.astype(f32)).astype(bf16)


def kernel(
    planes,
    sectors,
    ch,
    inner_ref,
    outer_ref,
    energy_ref,
    dipole_ref,
    surface_ref,
    threshold_ref,
    coef_ref,
    pattern_ref,
    size_ref,
    field_ref,
    inner_out,
    outer_out,
    dip_hi,
    dip_lo,
    mix_split,
    grid,
    term,
    peer_in,
    above_in,
    part_out,
    part_in,
    below_in,
    pairs,
    dip_full,
    live_ref,
    energy_rows,
    total_inner,
    diag_ref,
    edge_in,
    sem_e_send,
    sem_e_recv,
    sem_load,
    sem_g_send,
    sem_g_recv,
    sem_a_send,
    sem_a_recv,
    sem_z_send,
    sem_z_recv,
    sem_b_send,
    sem_b_recv,
    sem_y_send,
    sem_y_recv,
    sem_up_send,
    sem_up_recv,
    sem_down_send,
    sem_down_recv,
):
    z = lax.axis_index("inner")
    me = lax.axis_index("outer")
    blocks, rc = energy_ref.shape
    rows = 2 * blocks
    nc, nr = outer_ref.shape[1:]
    total = rc * sectors
    width = edge_in.shape[3]
    has_below = z > 0
    has_above = z < planes - 1

    @pl.when(z == 0)
    def _():
        below_in[...] = jnp.zeros_like(below_in)
        grid[:, :, 0:ch, :] = jnp.zeros((2, 2, ch, nr), f32)

    @pl.when(z == planes - 1)
    def _():
        above_in[...] = jnp.zeros_like(above_in)
        grid[:, :, ch + nc : 2 * ch + nc, :] = jnp.zeros((2, 2, ch, nr), f32)

    loads = [
        pltpu.make_async_copy(
            dipole_ref.at[pl.ds(l * rc, rc)], dip_full.at[pl.ds(l * rc, rc)], sem_load.at[l]
        )
        for l in range(blocks)
    ]
    for load in loads:
        load.start()

    for p in (1, 0):
        x = outer_ref[p]
        grid[0, p, ch : ch + nc, :] = x
        outer_out[p] = x

    def channel_copies(slot, p):
        up = pltpu.make_async_remote_copy(
            src_ref=grid.at[slot, p, pl.ds(nc, ch), :],
            dst_ref=grid.at[slot, p, pl.ds(0, ch), :],
            send_sem=sem_up_send.at[p],
            recv_sem=sem_up_recv.at[slot, p],
            device_id={"inner": z + 1, "outer": me},
            device_id_type=MESH,
        )
        down = pltpu.make_async_remote_copy(
            src_ref=grid.at[slot, p, pl.ds(ch, ch), :],
            dst_ref=grid.at[slot, p, pl.ds(ch + nc, ch), :],
            send_sem=sem_down_send.at[p],
            recv_sem=sem_down_recv.at[slot, p],
            device_id={"inner": z - 1, "outer": me},
            device_id_type=MESH,
        )
        return up, down

    side = pairs.shape[1]
    for l in range(blocks + 1):
        pairs[l, ch:side, :] = jnp.zeros((side - ch, side), f32)
    for l in range(blocks):
        pairs[l + 1, 0:ch, :] = jnp.zeros((ch, side), f32)
        pairs[l + 1, 0:ch, 0:ch] = coef_ref[l] * pattern_ref[l].astype(f32)

    @pl.when(z == 0)
    def _():
        pairs[0, 0:ch, :] = jnp.zeros((ch, side), f32)

    share = pltpu.make_async_remote_copy(
        src_ref=pairs.at[blocks, pl.ds(0, ch), :],
        dst_ref=pairs.at[0, pl.ds(0, ch), :],
        send_sem=sem_g_send,
        recv_sem=sem_g_recv,
        device_id={"inner": z + 1, "outer": me},
        device_id_type=MESH,
    )

    @pl.when(has_above)
    def _():
        share.start()
        for p in (1, 0):
            channel_copies(0, p)[0].start()

    @pl.when(has_below)
    def _():
        for p in (1, 0):
            channel_copies(0, p)[1].start()

    order_of = [(l, p) for l in range(blocks) for p in range(2)]
    position = me * rc + lax.broadcasted_iota(jnp.int32, (1, rc), 1)
    live_ref[...] = jnp.concatenate(
        [jnp.where(position < size_ref[l], 1.0, 0.0) for l, p in order_of], axis=0
    )
    energy_rows[...] = jnp.concatenate([energy_ref[l : l + 1, :] for l, p in order_of], axis=0)
    term[...] = live_ref[...] * jnp.concatenate(
        [inner_ref[p, l : l + 1, :] for l, p in order_of], axis=0
    )
    total_inner[...] = term[...]

    eye = lax.broadcasted_iota(jnp.int32, (nc, width), 0) == lax.broadcasted_iota(
        jnp.int32, (nc, width), 1
    )

    def to_row(col):
        return jnp.sum(jnp.where(eye, col, 0.0), axis=0, keepdims=True)

    def to_col(row):
        return jnp.sum(jnp.where(eye, row, 0.0), axis=1, keepdims=True)

    def wait(ref, sem):
        pltpu.make_async_copy(ref, ref, sem).wait()

    small = lax.broadcasted_iota(jnp.int32, (nc, nc), 0) == lax.broadcasted_iota(
        jnp.int32, (nc, nc), 1
    )
    diag_ref[...] = 2.0 * kinetic_scale + jnp.sum(
        jnp.where(small, threshold_ref[...], 0.0), axis=1, keepdims=True
    )

    def split_rows(i, carry):
        at = pl.ds(pl.multiple_of(i * 16, 16), 16)
        high, low = split(dip_full[at, :])
        dip_hi[at, :] = high
        dip_lo[at, :] = low
        return carry

    for l in range(blocks):
        loads[l].wait()
        lax.fori_loop(l * (rc // 16), (l + 1) * (rc // 16), split_rows, 0)

    @pl.when(has_below)
    def _():
        share.wait_recv()

    @pl.when(has_above)
    def _():
        share.wait_send()

    reach = -(-(nc + 2 * ch) // 128) * 128
    fill = jnp.zeros((ch, reach - side), f32)
    mixed_rows = []
    for l in range(blocks):
        upward = jnp.concatenate([pairs[l + 1, 0:ch, :], fill], axis=1)
        downward = jnp.concatenate([pairs[l].T[0:ch], fill], axis=1)
        upward = pltpu.roll(upward, (l + 2) * ch, 1)
        if l:
            downward = pltpu.roll(downward, l * ch, 1)
        mixed_rows.append((upward + downward)[:, 0 : nc + 2 * ch])
    mh, ml = split(jnp.concatenate(mixed_rows, axis=0))
    mix_split[0:nc, :] = mh
    mix_split[nc : 2 * nc, :] = ml

    def apply(t, carry):
        par = lax.rem(t, 2)
        nxt = 1 - par
        order = lax.rem(t, ORDER)
        strength = field_ref[lax.div(t, ORDER)]
        factor = time_step / (order + 1).astype(f32)
        last = order == ORDER - 1

        c = term[...]
        peer_in[par, me, 0:rows, 0:rc] = c
        def send_a(s, k):
            to = lax.rem(me + s, sectors)
            pltpu.make_async_remote_copy(
                src_ref=peer_in.at[par, me],
                dst_ref=peer_in.at[par, me],
                send_sem=sem_a_send,
                recv_sem=sem_a_recv.at[par],
                device_id={"inner": z, "outer": to},
                device_id_type=MESH,
            ).start()
            return k

        lax.fori_loop(1, sectors, send_a, 0)

        @pl.when(has_below)
        def _():
            def send_z(s, k):
                to = lax.rem(me + s, sectors)
                pltpu.make_async_remote_copy(
                    src_ref=peer_in.at[par, me, pl.ds(0, 2), pl.ds(0, rc)],
                    dst_ref=above_in.at[par, me, pl.ds(0, 2)],
                    send_sem=sem_z_send,
                    recv_sem=sem_z_recv.at[par],
                    device_id={"inner": z - 1, "outer": to},
                    device_id_type=MESH,
                ).start()
                return k

            lax.fori_loop(0, sectors, send_z, 0)

        edge_rows = []
        for p in range(2):
            edge_rows.append(to_row(grid[par, p, ch : ch + nc, 0:1]))
        for p in range(2):
            edge_rows.append(to_row(grid[par, p, ch : ch + nc, nr - 1 : nr]))
        for p in range(2):
            spread = jnp.concatenate(
                [
                    jnp.broadcast_to(c[2 * l + p : 2 * l + p + 1], (ch, rc))
                    for l in range(blocks)
                ],
                axis=0,
            )
            edge_rows.append(
                to_row(jnp.sum(surface_ref[...] * spread, axis=1, keepdims=True))
            )
        edge_rows.append(jnp.zeros((2, width), f32))
        edge_in[par, me] = jnp.concatenate(edge_rows, axis=0)

        def edge_copy(s):
            to = lax.rem(me + s, sectors)
            need = (s == 1) | (s == sectors - 1) | (to == 0) | (me == 0)
            out = pltpu.make_async_remote_copy(
                src_ref=edge_in.at[par, me],
                dst_ref=edge_in.at[par, me],
                send_sem=sem_e_send.at[to],
                recv_sem=sem_e_recv.at[par, me],
                device_id={"inner": z, "outer": to},
                device_id_type=MESH,
            )
            return need, to, out

        def send_e(s, k):
            need, to, out = edge_copy(s)

            @pl.when(need)
            def _():
                out.start()

            return k

        lax.fori_loop(1, sectors, send_e, 0)

        row_block = lax.broadcasted_iota(jnp.int32, (rows, 1), 0) // 2
        ch_, cl_ = split(c)
        both = jnp.concatenate([ch_, cl_], axis=0)
        back = jnp.zeros((rows, total), f32)
        for l in range(blocks):
            at = pl.ds(l * rc, rc)
            r = lax.dot_general(both, dip_hi[at, :], NN, preferred_element_type=f32)
            q = lax.dot_general(ch_, dip_lo[at, :], NN, preferred_element_type=f32)
            back = jnp.where(row_block == l, r[:rows] + r[rows:] + q, back)
        back = pltpu.roll(back, 2, 0)
        for k in range(sectors):
            part_out[k] = back[:, k * rc : (k + 1) * rc]
        part_in[par, me] = part_out[me]

        @pl.when(has_above)
        def _():
            def send_y(s, k):
                to = lax.rem(me + s, sectors)
                pltpu.make_async_remote_copy(
                    src_ref=part_out.at[to, pl.ds(0, 2)],
                    dst_ref=below_in.at[par, me, pl.ds(0, 2)],
                    send_sem=sem_y_send,
                    recv_sem=sem_y_recv.at[par],
                    device_id={"inner": z + 1, "outer": to},
                    device_id_type=MESH,
                ).start()
                return k

            lax.fori_loop(0, sectors, send_y, 0)

        def send_b(s, k):
            to = lax.rem(me + s, sectors)
            pltpu.make_async_remote_copy(
                src_ref=part_out.at[to],
                dst_ref=part_in.at[par, me],
                send_sem=sem_b_send,
                recv_sem=sem_b_recv.at[par],
                device_id={"inner": z, "outer": to},
                device_id_type=MESH,
            ).start()
            return k

        lax.fori_loop(1, sectors, send_b, 0)

        wait(peer_in.at[par, pl.ds(0, sectors - 1)], sem_a_recv.at[par])

        def forward_rows(values, l):
            vh, vl = values
            at = pl.ds(l * rc, rc)
            r = lax.dot_general(
                jnp.concatenate([vh, vl], axis=0), dip_hi[at, :], NT, preferred_element_type=f32
            )
            q = lax.dot_general(vh, dip_lo[at, :], NT, preferred_element_type=f32)
            return r[:rows] + r[rows:] + q

        own = split(
            jnp.concatenate([peer_in[par, k, 0:rows, 0:rc] for k in range(sectors)], axis=1)
        )
        ahead = jnp.zeros((rows, rc), f32)
        for l in range(blocks - 1):
            ahead = jnp.where(row_block == l + 1, forward_rows(own, l), ahead)

        @pl.when(has_above)
        def _():
            wait(above_in.at[par, :, pl.ds(0, 2)], sem_z_recv.at[par])

        other = split(jnp.concatenate([above_in[par, k] for k in range(sectors)], axis=1))
        ahead = jnp.where(row_block == 0, forward_rows(other, blocks - 1), ahead)
        ahead = pltpu.roll(ahead, rows - 2, 0)

        def take_e(s, k):
            need, source, out = edge_copy(s)

            @pl.when(need)
            def _():
                wait(edge_in.at[par, source], sem_e_recv.at[par, source])
                out.wait_send()

            return k

        lax.fori_loop(1, sectors, take_e, 0)

        surf = []
        edge = edge_in[par, 0]
        for p in range(2):
            prod = surface_ref[...] * to_col(edge[p : p + 1])
            surf.append(
                [
                    jnp.sum(prod[l * ch : (l + 1) * ch], axis=0, keepdims=True)
                    for l in range(blocks)
                ]
            )
        surf = jnp.concatenate(
            [surf[p][l] for l in range(blocks) for p in range(2)], axis=0
        )

        bound = jnp.zeros((8, width), f32)
        for k in range(sectors):
            bound = bound + edge_in[par, k]
        before = edge_in[par, lax.rem(me + sectors - 1, sectors)]
        after = edge_in[par, lax.rem(me + 1, sectors)]
        lane = lax.broadcasted_iota(jnp.int32, (1, nr), 1)
        for p in (1, 0):
            up, down = channel_copies(par, p)

            @pl.when(has_below)
            def _():
                up.wait_recv()

            @pl.when(has_above)
            def _():
                down.wait_recv()

            gh, gl = split(grid[par, p])
            r = lax.dot_general(mix_split[...], gh, NN, preferred_element_type=f32)
            q = lax.dot_general(mix_split[0:nc, :], gl, NN, preferred_element_type=f32)
            coupled = r[:nc] + r[nc:] + q
            left_row = jnp.where(me == 0, bound[4 + p : 5 + p], before[2 + p : 3 + p])
            right_row = jnp.where(me == sectors - 1, 0.0, after[p : p + 1])
            left_col = to_col(left_row)
            right_col = to_col(right_row)
            x = grid[par, p, ch : ch + nc, :]
            left = jnp.where(lane == 0, left_col, pltpu.roll(x, 1, 1))
            right = jnp.where(lane == nr - 1, right_col, pltpu.roll(x, nr - 1, 1))
            image = diag_ref[...] * x - kinetic_scale * (left + right) + strength * coupled
            value = (factor if p == 1 else -factor) * image
            acc = outer_out[1 - p] + value
            outer_out[1 - p] = acc
            grid[nxt, 1 - p, ch : ch + nc, :] = jnp.where(last, acc, value)
            new_up, new_down = channel_copies(nxt, 1 - p)
            up_old, down_old = channel_copies(par, 1 - p)

            @pl.when(has_above)
            def _():
                up_old.wait_send()

            @pl.when(has_below)
            def _():
                down_old.wait_send()

            @pl.when(jnp.logical_and(has_above, t < STEPS * ORDER - 1))
            def _():
                new_up.start()

            @pl.when(jnp.logical_and(has_below, t < STEPS * ORDER - 1))
            def _():
                new_down.start()


        wait(part_in.at[par, pl.ds(0, sectors - 1)], sem_b_recv.at[par])

        @pl.when(has_below)
        def _():
            wait(below_in.at[par, :, pl.ds(0, 2)], sem_y_recv.at[par])

        near = part_in[par, 0]
        far = below_in[par, 0]
        for k in range(1, sectors):
            near = near + part_in[par, k]
            far = far + below_in[par, k]
        behind = jnp.where(row_block == 0, far, near)
        image = live_ref[...] * (
            energy_rows[...] * c + strength * (ahead + behind) - kinetic_scale * surf
        )
        even = lax.rem(lax.broadcasted_iota(jnp.int32, (rows, 1), 0), 2) == 0
        value = factor * jnp.where(
            even, pltpu.roll(image, rows - 1, 0), -pltpu.roll(image, 1, 0)
        )
        acc = total_inner[...] + value
        total_inner[...] = acc
        term[...] = jnp.where(last, acc, value)

        wait(peer_in.at[par, pl.ds(0, sectors - 1)], sem_a_send)
        wait(part_in.at[par, pl.ds(0, sectors - 1)], sem_b_send)

        @pl.when(has_below)
        def _():
            wait(above_in.at[par, :, pl.ds(0, 2)], sem_z_send)

        @pl.when(has_above)
        def _():
            wait(below_in.at[par, :, pl.ds(0, 2)], sem_y_send)

        return carry

    lax.fori_loop(0, STEPS * ORDER, apply, 0)
    final = total_inner[...]
    for p in range(2):
        inner_out[p] = jnp.concatenate(
            [final[2 * l + p : 2 * l + p + 1] for l in range(blocks)], axis=0
        )


def local(
    planes,
    sectors,
    inner_state,
    outer_state,
    energies,
    dipole,
    surface,
    thresholds,
    coupling_coef,
    coupling_pattern,
    block_sizes,
    field_strength,
):
    blocks, rc, total = dipole.shape
    ch = coupling_coef.shape[1]
    nc, nr = outer_state.shape[1:]
    rows = 2 * blocks
    width = max(rc, -(-nc // 128) * 128)
    vmem = pl.BlockSpec(memory_space=pltpu.VMEM)
    dma = pltpu.SemaphoreType.DMA
    smem = pl.BlockSpec(memory_space=pltpu.SMEM)
    side = -(-ch // 128) * 128
    return pl.pallas_call(
        functools.partial(kernel, planes, sectors, ch),
        out_shape=(
            jax.ShapeDtypeStruct((2, blocks, rc), f32),
            jax.ShapeDtypeStruct((2, nc, nr), f32),
        ),
        in_specs=[vmem] * 3
        + [pl.BlockSpec(memory_space=pltpu.HBM)]
        + [vmem] * 4
        + [smem] * 2,
        out_specs=(vmem, vmem),
        scratch_shapes=[
            pltpu.VMEM((blocks * rc, total), bf16),
            pltpu.VMEM((blocks * rc, total), bf16),
            pltpu.VMEM((2 * nc, nc + 2 * ch), bf16),
            pltpu.VMEM((2, 2, nc + 2 * ch, nr), f32),
            pltpu.VMEM((rows, rc), f32),
            pltpu.VMEM((2, sectors, rows, rc), f32),
            pltpu.VMEM((2, sectors, rows, rc), f32),
            pltpu.VMEM((sectors, rows, rc), f32),
            pltpu.VMEM((2, sectors, rows, rc), f32),
            pltpu.VMEM((2, sectors, rows, rc), f32),
            pltpu.VMEM((blocks + 1, side, side), f32),
            pltpu.VMEM((blocks * rc, total), f32),
            pltpu.VMEM((rows, rc), f32),
            pltpu.VMEM((rows, rc), f32),
            pltpu.VMEM((rows, rc), f32),
            pltpu.VMEM((nc, 1), f32),
            pltpu.VMEM((2, sectors, 8, width), f32),
            dma((sectors,)), dma((2, sectors)),
            dma((blocks,)), dma(()), dma(()),
            dma(()), dma((2,)), dma(()), dma((2,)),
            dma(()), dma((2,)), dma(()), dma((2,)),
            dma((2,)), dma((2, 2)), dma((2,)), dma((2, 2)),
        ],
        compiler_params=pltpu.CompilerParams(
            has_side_effects=True, vmem_limit_bytes=56 * 1024 * 1024
        ),
    )(
        inner_state,
        outer_state,
        energies,
        dipole.reshape(blocks * rc, total),
        surface.reshape(nc, rc),
        thresholds.reshape(1, nc),
        coupling_coef,
        coupling_pattern,
        block_sizes,
        field_strength,
    )


def solution(mesh):
    placed = (
        P(None, "inner", "outer"),
        P(None, "inner", "outer"),
        P("inner", "outer"),
        P("inner", "outer", None),
        P("inner", None, "outer"),
        P("inner"),
        P("inner", None, None),
        P("inner", None, None),
        P("inner"),
        P(),
    )
    return jax.shard_map(
        functools.partial(local, mesh.shape["inner"], mesh.shape["outer"]),
        mesh=mesh,
        in_specs=placed,
        out_specs=(P(None, "inner", "outer"), P(None, "inner", "outer")),
        check_vma=False,
    )
```

profile of v0, /device:TPU:0, one launch (start us, length us, event | category | flops | bytes accessed | tf_op | source)
XLA Modules:
  0.0 79.4 jit_solution(1823971366774465261)
XLA Ops:
  0.6 75.5 %shard_map.113 = (f32[2,4,256]{2,1,0:T(4,128)}, f32[2,160,512]{2,1,0:T(8,128)}) custom-call(f32[2,4,256]{2,1,0:T(4,128)} %inner_ref.1, f32[2,160,512]{2,1,0:T(8,128)} %outer_ref.1, f32[4,256]{1,0:T(4,128)} %energy_ref.1, f32[1024,2048]{1,0:T(8,128)} %bitcast.3, f32[160,256]{1,0:T(8,128)} %bitcast.4, f32[1,160]{1,0:T(1,128)} %bitcast.5, ...), custom_call_target="tpu_custom_call" | custom-call | tf_op jit(solution)/shard_map/pallas_call | solution.py:526
  76.2 1.3 %copy.14 = f32[2,4,256]{2,1,0:T(4,128)} copy(f32[2,4,256]{2,1,0:T(4,128)} %get-tuple-element.4) | data formatting | bytes 16384
  77.5 2.0 %copy.15 = f32[2,160,512]{2,1,0:T(8,128)} copy(f32[2,160,512]{2,1,0:T(8,128)} %get-tuple-element.5) | data formatting | bytes 1310720
where the time goes:
time: 79.7 us; the launch traced here: 79.4 us
  Pallas kernels  75.5 us (95%)
  local copies, waits for them, and re-layouts  3.26 us (4%)
    pallas_call x1, Pallas kernels, local(): pl.pallas_call(functools.partial(kernel, planes, sectors, ch), out_shape=...  75.5 us
    unnamed x2, local copies, waits for them, and re-layouts  3.26 us

commit v1 on v0

v1 whole, which is shorter than its diff:
```python
import functools

import jax
import jax.numpy as jnp
from jax import lax
from jax.experimental import pallas as pl
from jax.experimental.pallas import tpu as pltpu
from jax.sharding import PartitionSpec as P

STEPS = 2
ORDER = 4

kinetic_scale = 3.125
time_step = 0.1

MESH = pl.DeviceIdType.MESH
f32 = jnp.float32
bf16 = jnp.bfloat16
NN = (((1,), (0,)), ((), ()))
SLOTS = 4


def halves(x):
    high = x.astype(bf16).astype(f32)
    return high, x - high


def split(x):
    high = x.astype(bf16)
    return high, (x - high.astype(f32)).astype(bf16)


def dot(a, b):
    return lax.dot_general(a, b, NN, preferred_element_type=f32)


def kernel(
    planes,
    sectors,
    ch,
    inner_ref,
    outer_hbm,
    energy_ref,
    dipole_hbm,
    surface_ref,
    threshold_ref,
    coef_ref,
    pattern_ref,
    size_ref,
    field_ref,
    inner_out,
    outer_out,
    dip_full,
    dip_cat,
    dip_turn,
    surf_cat,
    surf_turn,
    mix_split,
    grid,
    halo_out,
    term,
    peer_in,
    first_out,
    above_in,
    part_out,
    part_in,
    far_out,
    below_in,
    pairs,
    live_ref,
    energy_rows,
    total_inner,
    diag_ref,
    edge_out,
    left_in,
    right_in,
    surf_in,
    point_in,
    sem_load,
    sem_outer,
    sem_g_send,
    sem_g_recv,
    sem_a_send,
    sem_a_recv,
    sem_z_send,
    sem_z_recv,
    sem_b_send,
    sem_b_recv,
    sem_y_send,
    sem_y_recv,
    sem_up_send,
    sem_up_recv,
    sem_down_send,
    sem_down_recv,
    sem_e_send,
    sem_left,
    sem_right,
    sem_surf_send,
    sem_surf,
    sem_point_send,
    sem_point,
):
    z = lax.axis_index("inner")
    me = lax.axis_index("outer")
    blocks, rc = energy_ref.shape
    rows = 2 * blocks
    nc, nr = grid.shape[2] - 2 * ch, grid.shape[3]
    ext = edge_out.shape[2]
    depth = 2 * blocks * rc
    near = rows - 2
    has_below = z > 0
    has_above = z < planes - 1
    power = sectors & (sectors - 1) == 0

    def partner(s):
        if not power:
            return lax.rem(me + s, sectors)
        to, bit = me, 1
        while bit < sectors:
            if s & bit:
                to = to + bit * (1 - 2 * ((me // bit) % 2))
            bit *= 2
        return to

    def source(s):
        return partner(s) if power else lax.rem(me + sectors - s, sectors)

    def remote(src, dst, send, recv, plane, sector):
        return pltpu.make_async_remote_copy(
            src_ref=src,
            dst_ref=dst,
            send_sem=send,
            recv_sem=recv,
            device_id={"inner": plane, "outer": sector},
            device_id_type=MESH,
        )

    def wait(ref, sem):
        pltpu.make_async_copy(ref, ref, sem).wait()

    barrier = pltpu.get_barrier_semaphore()

    def greet(plane, s):
        pl.semaphore_signal(
            barrier,
            inc=1,
            device_id={"inner": plane, "outer": partner(s)},
            device_id_type=MESH,
        )

    for s in range(sectors - 1, 0, -1):
        greet(z, s)

    @pl.when(has_below)
    def _():
        for s in range(sectors - 1, -1, -1):
            greet(z - 1, s)

    @pl.when(has_above)
    def _():
        for s in range(sectors - 1, -1, -1):
            greet(z + 1, s)

    own = pl.ds(ch, nc)
    states = []
    for p in range(2):
        states.append(
            pltpu.make_async_copy(outer_hbm.at[p], grid.at[0, p, own, :], sem_outer.at[p])
        )
        states.append(
            pltpu.make_async_copy(
                outer_hbm.at[p, pl.ds(nc - ch, ch)], halo_out.at[p, 0], sem_outer.at[2 + p]
            )
        )
        states.append(
            pltpu.make_async_copy(
                outer_hbm.at[p, pl.ds(0, ch)], halo_out.at[p, 1], sem_outer.at[4 + p]
            )
        )
        states.append(
            pltpu.make_async_copy(outer_hbm.at[p], outer_out.at[p], sem_outer.at[6 + p])
        )
    for state in states:
        state.start()
    loads = [
        pltpu.make_async_copy(
            dipole_hbm.at[pl.ds(l * rc, rc)], dip_full.at[pl.ds(l * rc, rc)], sem_load.at[l]
        )
        for l in range(blocks)
    ]
    for load in loads:
        load.start()

    @pl.when(z == 0)
    def _():
        below_in[...] = jnp.zeros_like(below_in)
        grid[:, :, 0:ch, :] = jnp.zeros((2, 2, ch, nr), f32)

    @pl.when(z == planes - 1)
    def _():
        above_in[...] = jnp.zeros_like(above_in)
        grid[:, :, ch + nc : 2 * ch + nc, :] = jnp.zeros((2, 2, ch, nr), f32)

    def channel_copies(slot, p):
        up = remote(
            halo_out.at[p, 0],
            grid.at[slot, p, pl.ds(0, ch), :],
            sem_up_send.at[p],
            sem_up_recv.at[slot, p],
            z + 1,
            me,
        )
        down = remote(
            halo_out.at[p, 1],
            grid.at[slot, p, pl.ds(ch + nc, ch), :],
            sem_down_send.at[p],
            sem_down_recv.at[slot, p],
            z - 1,
            me,
        )
        return up, down

    side = pairs.shape[1]
    for l in range(blocks + 1):
        pairs[l, ch:side, :] = jnp.zeros((side - ch, side), f32)
    for l in range(blocks):
        pairs[l + 1, 0:ch, :] = jnp.zeros((ch, side), f32)
        pairs[l + 1, 0:ch, 0:ch] = coef_ref[l] * pattern_ref[l].astype(f32)

    @pl.when(z == 0)
    def _():
        pairs[0, 0:ch, :] = jnp.zeros((ch, side), f32)

    share = remote(
        pairs.at[blocks, pl.ds(0, ch), :],
        pairs.at[0, pl.ds(0, ch), :],
        sem_g_send,
        sem_g_recv,
        z + 1,
        me,
    )

    order_of = [(l, p) for l in range(blocks) for p in range(2)]
    position = me * rc + lax.broadcasted_iota(jnp.int32, (1, rc), 1)
    live_ref[...] = jnp.concatenate(
        [jnp.where(position < size_ref[l], 1.0, 0.0) for l, p in order_of], axis=0
    )
    energy_rows[...] = jnp.concatenate([energy_ref[l : l + 1, :] for l, p in order_of], axis=0)
    term[...] = live_ref[...] * jnp.concatenate(
        [inner_ref[p, l : l + 1, :] for l, p in order_of], axis=0
    )
    total_inner[...] = term[...]

    small = lax.broadcasted_iota(jnp.int32, (nc, nc), 0) == lax.broadcasted_iota(
        jnp.int32, (nc, nc), 1
    )
    diag_ref[...] = 2.0 * kinetic_scale + jnp.sum(
        jnp.where(small, threshold_ref[...], 0.0), axis=1, keepdims=True
    )

    surface_ext = jnp.concatenate(
        [
            jnp.zeros((ch, rc), f32),
            surface_ref[...],
            jnp.zeros((ext - ch - nc, rc), f32),
        ],
        axis=0,
    )
    sh, sl = split(surface_ext)
    surf_cat[0:ext, :] = sh
    surf_cat[ext : 2 * ext, :] = sl
    surf_turn[0:rc, :] = sh.T
    surf_turn[rc : 2 * rc, :] = sl.T

    waits = (sectors - 1) + sectors * (
        jnp.where(has_below, 1, 0) + jnp.where(has_above, 1, 0)
    )
    pl.semaphore_wait(barrier, waits)

    @pl.when(has_above)
    def _():
        share.start()

    for p in (1, 0):
        states[4 * p + 1].wait()
        states[4 * p + 2].wait()
        up, down = channel_copies(0, p)

        @pl.when(has_above)
        def _():
            up.start()

        @pl.when(has_below)
        def _():
            down.start()

    for l in range(blocks):
        loads[l].wait()

        def turn(k, carry):
            at = pl.ds(pl.multiple_of(k * rc, 128), rc)
            high, low = split(dip_full[l * rc : (l + 1) * rc, at])
            dip_cat[2 * l * rc : (2 * l + 1) * rc, at] = high
            dip_cat[(2 * l + 1) * rc : (2 * l + 2) * rc, at] = low
            base = k * depth + 2 * l * rc
            dip_turn[pl.ds(pl.multiple_of(base, 128), rc), :] = high.T
            dip_turn[pl.ds(pl.multiple_of(base + rc, 128), rc), :] = low.T
            return carry

        lax.fori_loop(0, sectors, turn, 0)

    @pl.when(has_below)
    def _():
        share.wait_recv()

    @pl.when(has_above)
    def _():
        share.wait_send()

    reach = -(-(nc + 2 * ch) // 128) * 128
    fill = jnp.zeros((ch, reach - side), f32)
    mixed_rows = []
    for l in range(blocks):
        upward = jnp.concatenate([pairs[l + 1, 0:ch, :], fill], axis=1)
        downward = jnp.concatenate([pairs[l].T[0:ch], fill], axis=1)
        upward = pltpu.roll(upward, (l + 2) * ch, 1)
        if l:
            downward = pltpu.roll(downward, l * ch, 1)
        mixed_rows.append((upward + downward)[:, 0 : nc + 2 * ch])
    mh, ml = split(jnp.concatenate(mixed_rows, axis=0))
    mix_split[0:nc, :] = mh
    mix_split[nc : 2 * nc, :] = ml
    for p in range(2):
        states[4 * p].wait()
        states[4 * p + 3].wait()

    row_block = lax.broadcasted_iota(jnp.int32, (rows, 1), 0) // 2
    low_lane = ch + ch * (lax.broadcasted_iota(jnp.int32, (rows, ext), 0) // 2)
    lane_of = lax.broadcasted_iota(jnp.int32, (rows, ext), 1)
    own_lanes = (lane_of >= low_lane) & (lane_of < low_lane + ch)

    def eye(count, shift):
        return (
            lax.broadcasted_iota(jnp.int32, (count, ext), 0) + shift
            == lax.broadcasted_iota(jnp.int32, (count, ext), 1)
        )

    def to_row(col):
        return jnp.sum(jnp.where(eye(nc, ch), col, 0.0), axis=0, keepdims=True)

    def to_col(row, count, shift):
        return jnp.sum(jnp.where(eye(count, shift), row, 0.0), axis=1, keepdims=True)

    def spread(v, first, count):
        high, low = halves(v)
        zero = jnp.zeros_like(v)
        top, bottom = [], []
        for l in range(first, first + count):
            mine = row_block == l
            h = jnp.where(mine, high, 0.0)
            top += [h, h]
            bottom += [jnp.where(mine, low, 0.0), zero]
        return jnp.concatenate(
            [jnp.concatenate(top, axis=1), jnp.concatenate(bottom, axis=1)], axis=0
        ).astype(bf16)

    def stacked(v):
        high, low = halves(v)
        return jnp.concatenate(
            [
                jnp.concatenate([high, high], axis=1),
                jnp.concatenate([low, jnp.zeros_like(low)], axis=1),
            ],
            axis=0,
        ).astype(bf16)

    def fold(r):
        return r[:rows] + r[rows:]

    def edge_sends(st, f):
        def three(cond, src, dst, sem, send, sector):
            @pl.when(cond)
            def _():
                f(remote(src, dst(0), send.at[0], sem.at[st, 0], z, sector))

                @pl.when(has_below)
                def _():
                    f(remote(src, dst(2), send.at[1], sem.at[st, 2], z - 1, sector))

                @pl.when(has_above)
                def _():
                    f(remote(src, dst(1), send.at[2], sem.at[st, 1], z + 1, sector))

        three(
            me > 0,
            edge_out.at[st, pl.ds(0, 2)],
            lambda o: right_in.at[st, o, pl.ds(0, 2)],
            sem_right,
            sem_e_send.at[0],
            me - 1,
        )
        three(
            me < sectors - 1,
            edge_out.at[st + SLOTS, pl.ds(0, 2)],
            lambda o: left_in.at[st, o, pl.ds(0, 2)],
            sem_left,
            sem_e_send.at[1],
            me + 1,
        )

    def surf_sends(st, f):
        src = surf_in.at[st, 0, me, pl.ds(0, 2)]

        @pl.when(me > 0)
        def _():
            f(remote(src, src, sem_surf_send.at[0], sem_surf.at[st, 0], z, 0))

        @pl.when(has_below)
        def _():
            dst = surf_in.at[st, 2, me, pl.ds(0, 2)]
            f(remote(src, dst, sem_surf_send.at[1], sem_surf.at[st, 2], z - 1, 0))

        @pl.when(has_above)
        def _():
            dst = surf_in.at[st, 1, me, pl.ds(0, 2)]
            f(remote(src, dst, sem_surf_send.at[2], sem_surf.at[st, 1], z + 1, 0))

    def point_sends(st, f):
        @pl.when(me == 0)
        def _():
            src = point_in.at[st, pl.ds(0, 2)]
            for k in range(1, sectors):
                f(remote(src, src, sem_point_send.at[k], sem_point.at[st], z, k))

    def edge_waits(sl):
        def each(f):
            f(0)

            @pl.when(has_below)
            def _():
                f(1)

            @pl.when(has_above)
            def _():
                f(2)

        @pl.when(me > 0)
        def _():
            each(lambda o: wait(left_in.at[sl, o, pl.ds(0, 2)], sem_left.at[sl, o]))

        @pl.when(me < sectors - 1)
        def _():
            each(lambda o: wait(right_in.at[sl, o, pl.ds(0, 2)], sem_right.at[sl, o]))

        @pl.when(me == 0)
        def _():
            each(
                lambda o: wait(
                    surf_in.at[sl, o, pl.ds(1 if o == 0 else 0, sectors - (o == 0)), pl.ds(0, 2)],
                    sem_surf.at[sl, o],
                )
            )

    def edge_rows(sl, o):
        total_b = surf_in[sl, o, 0]
        for k in range(1, sectors):
            total_b = total_b + surf_in[sl, o, k]
        left = jnp.where(me == 0, total_b, left_in[sl, o])
        right = jnp.where(me == sectors - 1, 0.0, right_in[sl, o])
        if o == 1:
            left, right = jnp.where(has_below, left, 0.0), jnp.where(has_below, right, 0.0)
        if o == 2:
            left, right = jnp.where(has_above, left, 0.0), jnp.where(has_above, right, 0.0)
        return left, right

    lane = lax.broadcasted_iota(jnp.int32, (1, 128), 1)

    def scales(t):
        order = lax.rem(t, ORDER)
        factor = time_step / (order + 1).astype(f32)
        return factor * kinetic_scale, -factor * kinetic_scale

    def correct_own(t, par, refresh):
        sl = lax.rem(t, SLOTS)
        left, right = edge_rows(sl, 0)
        for d, scale in ((1, scales(t)[0]), (0, scales(t)[1])):
            first = jnp.where(lane == 0, scale * to_col(left[1 - d : 2 - d], nc, ch), 0.0)
            last = jnp.where(lane == 127, scale * to_col(right[1 - d : 2 - d], nc, ch), 0.0)
            outer_out[d, :, 0:128] += first
            outer_out[d, :, nr - 128 : nr] += last
            if refresh:
                grid[par, d, own, 0:128] += first
                grid[par, d, own, nr - 128 : nr] += last

    def apply(t, carry):
        par = lax.rem(t, 2)
        nxt = 1 - par
        st = lax.rem(t, SLOTS)
        order = lax.rem(t, ORDER)
        strength = field_ref[lax.div(t, ORDER)]
        factor = time_step / (order + 1).astype(f32)
        last = order == ORDER - 1

        c = term[...]
        shifted = pltpu.roll(c, rows - 2, 0)
        peer_in[par, me] = shifted
        first_out[par] = c
        copies = []
        for s in range(sectors - 1, 0, -1):
            here = peer_in.at[par, me, pl.ds(0, near)]
            copies.append(
                remote(here, here, sem_a_send.at[s], sem_a_recv.at[par, s], z, partner(s))
            )
        z_copies = [
            remote(
                first_out.at[par, pl.ds(0, 2)],
                above_in.at[par, me, pl.ds(0, 2)],
                sem_z_send.at[s],
                sem_z_recv.at[par, s],
                z - 1,
                partner(s),
            )
            for s in range(sectors - 1, -1, -1)
        ]

        @pl.when(has_below)
        def _():
            for copy in z_copies:
                copy.start()

        for copy in copies:
            copy.start()

        b = fold(dot(stacked(c), surf_turn[...]))
        b = jnp.where(own_lanes, b, 0.0)
        total_b = b
        for l in range(1, blocks):
            total_b = total_b + pltpu.roll(b, 2 * l, 0)
        surf_in[st, 0, me] = total_b
        surf_sends(st, lambda copy: copy.start())

        lhs = stacked(c)
        y_copies, b_copies = [], []
        for s in range(sectors - 1, -1, -1):
            to = partner(s)
            at = pl.ds(pl.multiple_of(to * rc, 128), rc)
            back = jnp.zeros((rows, rc), f32)
            for l in range(blocks):
                r = fold(dot(lhs, dip_cat[2 * l * rc : 2 * (l + 1) * rc, at]))
                back = jnp.where(row_block == l, r, back)
            if s:
                part_out[s] = back
                b_copies.append(
                    remote(
                        part_out.at[s, pl.ds(0, near)],
                        part_in.at[par, me, pl.ds(0, near)],
                        sem_b_send.at[s],
                        sem_b_recv.at[par, s],
                        z,
                        to,
                    )
                )
            else:
                part_in[par, me] = back
            far_out[s] = pltpu.roll(back, 2, 0)
            y_copies.append(
                remote(
                    far_out.at[s, pl.ds(0, 2)],
                    below_in.at[par, me, pl.ds(0, 2)],
                    sem_y_send.at[s],
                    sem_y_recv.at[par, s],
                    z + 1,
                    to,
                )
            )
            if s % 2 == 0:

                @pl.when(has_above)
                def _():
                    for copy in y_copies[-2:]:
                        copy.start()

                for copy in b_copies[-2:] if s else b_copies[-1:]:
                    copy.start()

        @pl.when(t > 0)
        def _():
            edge_waits(lax.rem(t + SLOTS - 1, SLOTS))
            correct_own(t - 1, par, True)

        for e in range(2):
            edges = []
            for p in range(2):
                x = grid[par, p, own, nr - 128 : nr] if e else grid[par, p, own, 0:128]
                edges.append(to_row(x[:, 127:128] if e else x[:, 0:1]))
            edges.append(jnp.zeros((6, ext), f32))
            edge_out[st + e * SLOTS] = jnp.concatenate(edges, axis=0)

        @pl.when(me == 0)
        def _():
            point_in[st] = edge_out[st]

        point_sends(st, lambda copy: copy.start())
        edge_sends(st, lambda copy: copy.start())

        def unit(q):
            p = lax.rem(t + 1 + q, 2)
            imag = p == 1
            up, down = channel_copies(par, p)

            @pl.when(has_below)
            def _():
                up.wait_recv()

            @pl.when(has_above)
            def _():
                down.wait_recv()

            @pl.when(t > 0)
            def _():
                sl = lax.rem(t + SLOTS - 1, SLOTS)
                one, zero = scales(t - 1)
                scale = jnp.where(imag, one, zero)
                for o, start, shift in ((1, 0, nc), (2, ch + nc, ch)):
                    left, right = edge_rows(sl, o)
                    left = jnp.where(imag, left[0:1], left[1:2])
                    right = jnp.where(imag, right[0:1], right[1:2])
                    at = pl.ds(start, ch)
                    grid[par, p, at, 0:128] += jnp.where(
                        lane == 0, scale * to_col(left, ch, shift), 0.0
                    )
                    grid[par, p, at, nr - 128 : nr] += jnp.where(
                        lane == 127, scale * to_col(right, ch, shift), 0.0
                    )

            gh, gl = split(grid[par, p])
            r = dot(mix_split[...], gh)
            coupled = r[:nc] + r[nc:] + dot(mix_split[0:nc, :], gl)
            x = grid[par, p, own, :]
            lanes = lax.broadcasted_iota(jnp.int32, (1, nr), 1)
            left = jnp.where(lanes == 0, 0.0, pltpu.roll(x, 1, 1))
            right = jnp.where(lanes == nr - 1, 0.0, pltpu.roll(x, nr - 1, 1))
            image = diag_ref[...] * x - kinetic_scale * (left + right) + strength * coupled
            value = jnp.where(imag, factor, -factor) * image
            acc = outer_out[1 - p] + value
            outer_out[1 - p] = acc
            value = jnp.where(last, acc, value)
            up_old, down_old = channel_copies(par, 1 - p)

            @pl.when(has_above)
            def _():
                up_old.wait_send()

            @pl.when(has_below)
            def _():
                down_old.wait_send()

            grid[nxt, 1 - p, own, :] = value
            halo_out[1 - p, 0] = value[nc - ch : nc]
            halo_out[1 - p, 1] = value[0:ch]
            up_new, down_new = channel_copies(nxt, 1 - p)

            @pl.when(jnp.logical_and(has_above, t < STEPS * ORDER - 1))
            def _():
                up_new.start()

            @pl.when(jnp.logical_and(has_below, t < STEPS * ORDER - 1))
            def _():
                down_new.start()

        def take(groups, first, count):
            for s in groups:
                if s and first == 0:
                    wait(peer_in.at[par, source(s), pl.ds(0, near)], sem_a_recv.at[par, s])
            total = jnp.zeros((rows, rc), f32)
            for group in (groups[0::2], groups[1::2]):
                sums = [None] * count
                for s in group:
                    k = source(s)
                    if first:
                        left = stacked(pltpu.roll(above_in[par, k], rows - 2, 0))
                    else:
                        left = stacked(peer_in[par, k])
                    for i in range(count):
                        base = k * depth + 2 * (first + i) * rc
                        at = pl.ds(pl.multiple_of(base, 128), 2 * rc)
                        part = dot(left, dip_turn[at, :])
                        sums[i] = part if sums[i] is None else sums[i] + part
                for i in range(count):
                    total = total + jnp.where(row_block == first + i, fold(sums[i]), 0.0)
            return total

        unit(0)
        ahead = take([0, 1], 0, blocks - 1)
        middle = list(range(2, sectors * 3 // 4))
        tail = list(range(sectors * 3 // 4, sectors))
        unit(1)
        ahead = ahead + take(middle, 0, blocks - 1)
        ahead = ahead + take(tail, 0, blocks - 1)

        @pl.when(me > 0)
        def _():
            wait(point_in.at[st, pl.ds(0, 2)], sem_point.at[st])

        point = jnp.concatenate([point_in[st, 0:2]] * blocks, axis=0)
        surf = fold(dot(stacked(jnp.where(own_lanes, point, 0.0)), surf_cat[...]))

        for s in range(1, sectors):
            wait(part_in.at[par, source(s), pl.ds(0, near)], sem_b_recv.at[par, s])
        behind = part_in[par, 0]
        for k in range(1, sectors):
            behind = behind + part_in[par, k]

        @pl.when(has_above)
        def _():
            for s in range(sectors):
                wait(above_in.at[par, source(s), pl.ds(0, 2)], sem_z_recv.at[par, s])

        ahead = ahead + take(list(range(sectors)), blocks - 1, 1)

        @pl.when(has_below)
        def _():
            for s in range(sectors):
                wait(below_in.at[par, source(s), pl.ds(0, 2)], sem_y_recv.at[par, s])

        far = below_in[par, 0]
        for k in range(1, sectors):
            far = far + below_in[par, k]
        behind = jnp.where(row_block == 0, far, pltpu.roll(behind, 2, 0))
        image = live_ref[...] * (
            energy_rows[...] * c + strength * (ahead + behind) - kinetic_scale * surf
        )
        even = lax.rem(lax.broadcasted_iota(jnp.int32, (rows, 1), 0), 2) == 0
        value = factor * jnp.where(
            even, pltpu.roll(image, rows - 1, 0), -pltpu.roll(image, 1, 0)
        )
        acc = total_inner[...] + value
        total_inner[...] = acc
        term[...] = jnp.where(last, acc, value)

        for copy in copies + b_copies:
            copy.wait_send()

        @pl.when(has_below)
        def _():
            for copy in z_copies:
                copy.wait_send()

        @pl.when(has_above)
        def _():
            for copy in y_copies:
                copy.wait_send()

        surf_sends(st, lambda copy: copy.wait_send())
        point_sends(st, lambda copy: copy.wait_send())
        edge_sends(st, lambda copy: copy.wait_send())
        return carry

    count = STEPS * ORDER
    lax.fori_loop(0, count, apply, 0)
    edge_waits((count - 1) % SLOTS)
    correct_own(jnp.int32(count - 1), 0, False)
    final = total_inner[...]
    for p in range(2):
        inner_out[p] = jnp.concatenate(
            [final[2 * l + p : 2 * l + p + 1] for l in range(blocks)], axis=0
        )


def local(
    planes,
    sectors,
    inner_state,
    outer_state,
    energies,
    dipole,
    surface,
    thresholds,
    coupling_coef,
    coupling_pattern,
    block_sizes,
    field_strength,
):
    blocks, rc, total = dipole.shape
    ch = coupling_coef.shape[1]
    nc, nr = outer_state.shape[1:]
    rows = 2 * blocks
    ext = -(-(nc + 2 * ch) // 128) * 128
    vmem = pl.BlockSpec(memory_space=pltpu.VMEM)
    hbm = pl.BlockSpec(memory_space=pltpu.HBM)
    dma = pltpu.SemaphoreType.DMA
    smem = pl.BlockSpec(memory_space=pltpu.SMEM)
    side = -(-ch // 128) * 128
    return pl.pallas_call(
        functools.partial(kernel, planes, sectors, ch),
        out_shape=(
            jax.ShapeDtypeStruct((2, blocks, rc), f32),
            jax.ShapeDtypeStruct((2, nc, nr), f32),
        ),
        in_specs=[vmem, hbm, vmem, hbm] + [vmem] * 4 + [smem] * 2,
        out_specs=(vmem, vmem),
        scratch_shapes=[
            pltpu.VMEM((blocks * rc, total), f32),
            pltpu.VMEM((2 * blocks * rc, total), bf16),
            pltpu.VMEM((2 * blocks * total, rc), bf16),
            pltpu.VMEM((2 * ext, rc), bf16),
            pltpu.VMEM((2 * rc, ext), bf16),
            pltpu.VMEM((2 * nc, nc + 2 * ch), bf16),
            pltpu.VMEM((2, 2, nc + 2 * ch, nr), f32),
            pltpu.VMEM((2, 2, ch, nr), f32),
            pltpu.VMEM((rows, rc), f32),
            pltpu.VMEM((2, sectors, rows, rc), f32),
            pltpu.VMEM((2, rows, rc), f32),
            pltpu.VMEM((2, sectors, rows, rc), f32),
            pltpu.VMEM((sectors, rows, rc), f32),
            pltpu.VMEM((2, sectors, rows, rc), f32),
            pltpu.VMEM((sectors, rows, rc), f32),
            pltpu.VMEM((2, sectors, rows, rc), f32),
            pltpu.VMEM((blocks + 1, side, side), f32),
            pltpu.VMEM((rows, rc), f32),
            pltpu.VMEM((rows, rc), f32),
            pltpu.VMEM((rows, rc), f32),
            pltpu.VMEM((nc, 1), f32),
            pltpu.VMEM((2 * SLOTS, 8, ext), f32),
            pltpu.VMEM((SLOTS, 3, 8, ext), f32),
            pltpu.VMEM((SLOTS, 3, 8, ext), f32),
            pltpu.VMEM((SLOTS, 3, sectors, 8, ext), f32),
            pltpu.VMEM((SLOTS, 8, ext), f32),
            dma((blocks,)), dma((8,)), dma(()), dma(()),
            dma((sectors,)), dma((2, sectors)),
            dma((sectors,)), dma((2, sectors)),
            dma((sectors,)), dma((2, sectors)),
            dma((sectors,)), dma((2, sectors)),
            dma((2,)), dma((2, 2)), dma((2,)), dma((2, 2)),
            dma((2, 3)), dma((SLOTS, 3)), dma((SLOTS, 3)),
            dma((3,)), dma((SLOTS, 3)),
            dma((sectors,)), dma((SLOTS,)),
        ],
        compiler_params=pltpu.CompilerParams(
            collective_id=0, has_side_effects=True, vmem_limit_bytes=56 * 1024 * 1024
        ),
    )(
        inner_state,
        outer_state,
        energies,
        dipole.reshape(blocks * rc, total),
        surface.reshape(nc, rc),
        thresholds.reshape(1, nc),
        coupling_coef,
        coupling_pattern,
        block_sizes,
        field_strength,
    )
def solution(mesh):
    placed = (
        P(None, "inner", "outer"),
        P(None, "inner", "outer"),
        P("inner", "outer"),
        P("inner", "outer", None),
        P("inner", None, "outer"),
        P("inner"),
        P("inner", None, None),
        P("inner", None, None),
        P("inner"),
        P(),
    )
    return jax.shard_map(
        functools.partial(local, mesh.shape["inner"], mesh.shape["outer"]),
        mesh=mesh,
        in_specs=placed,
        out_specs=(P(None, "inner", "outer"), P(None, "inner", "outer")),
        check_vma=False,
    )
```

time: 79.7 us -> 61.9 us (0.78)
  Pallas kernels: 75.5 us -> 57.7 us
    pallas_call x1, Pallas kernels: 75.5 us -> 57.7 us  [local(): pl.pallas_call(functools.partial(kernel, planes, sectors, ch), out_shape=...]
where the time goes in v1:
time: 61.9 us; the launch traced here: 61.6 us
  Pallas kernels  57.7 us (93%)
  local copies, waits for them, and re-layouts  3.26 us (5%)
  between operations  0.64 us (1%)
    pallas_call x1, Pallas kernels, local(): pl.pallas_call(functools.partial(kernel, planes, sectors, ch), out_shape=...  57.7 us
    unnamed x2, local copies, waits for them, and re-layouts  3.26 us

profile of v1, /device:TPU:0, one launch (start us, length us, event | category | flops | bytes accessed | tf_op | source)
XLA Modules:
  0.0 61.6 jit_solution(5538297322255192784)
XLA Ops:
  0.6 57.7 %shard_map.113 = (f32[2,4,256]{2,1,0:T(4,128)}, f32[2,160,512]{2,1,0:T(8,128)}) custom-call(f32[2,4,256]{2,1,0:T(4,128)} %inner_ref.1, f32[2,160,512]{2,1,0:T(8,128)} %outer_hbm.1, f32[4,256]{1,0:T(4,128)} %energy_ref.1, f32[1024,2048]{1,0:T(8,128)} %bitcast.3, f32[160,256]{1,0:T(8,128)} %bitcast.4, f32[1,160]{1,0:T(1,128)} %bitcast.5, ...), custom_call_target="tpu_custom_call" | custom-call | tf_op jit(solution)/shard_map/pallas_call | solution.py:794
  58.4 1.3 %copy.14 = f32[2,4,256]{2,1,0:T(4,128)} copy(f32[2,4,256]{2,1,0:T(4,128)} %get-tuple-element.4) | data formatting | bytes 16384
  59.7 2.0 %copy.15 = f32[2,160,512]{2,1,0:T(8,128)} copy(f32[2,160,512]{2,1,0:T(8,128)} %get-tuple-element.5) | data formatting | bytes 1310720

commit v2 on v1

v2 whole, which is shorter than its diff:
```python
import functools

import jax
import jax.numpy as jnp
from jax import lax
from jax.experimental import pallas as pl
from jax.experimental.pallas import tpu as pltpu
from jax.sharding import PartitionSpec as P

STEPS = 2
ORDER = 4

kinetic_scale = 3.125
time_step = 0.1

MESH = pl.DeviceIdType.MESH
f32 = jnp.float32
bf16 = jnp.bfloat16
NN = (((1,), (0,)), ((), ()))
SLOTS = 4


def halves(x):
    high = x.astype(bf16).astype(f32)
    return high, x - high


def split(x):
    high = x.astype(bf16)
    return high, (x - high.astype(f32)).astype(bf16)


def dot(a, b):
    return lax.dot_general(a, b, NN, preferred_element_type=f32)


def kernel(
    planes,
    sectors,
    ch,
    inner_hbm,
    outer_hbm,
    energy_hbm,
    dipole_hbm,
    surface_hbm,
    threshold_hbm,
    coef_hbm,
    pattern_hbm,
    size_hbm,
    field_hbm,
    inner_out,
    outer_out,
    inner_ref,
    energy_ref,
    surface_ref,
    threshold_ref,
    coef_ref,
    pattern_ref,
    size_ref,
    field_ref,
    sem_small,
    dip_full,
    dip_cat,
    dip_turn,
    surf_cat,
    surf_turn,
    mix_split,
    grid,
    halo_out,
    term,
    peer_in,
    first_out,
    above_in,
    part_out,
    part_in,
    far_out,
    below_in,
    pairs,
    live_ref,
    energy_rows,
    total_inner,
    diag_ref,
    raw_rows,
    edge_out,
    left_in,
    right_in,
    surf_in,
    point_in,
    sem_load,
    sem_outer,
    sem_g_send,
    sem_g_recv,
    sem_a_send,
    sem_a_recv,
    sem_z_send,
    sem_z_recv,
    sem_b_send,
    sem_b_recv,
    sem_y_send,
    sem_y_recv,
    sem_up_send,
    sem_up_recv,
    sem_down_send,
    sem_down_recv,
    sem_e_send,
    sem_left,
    sem_right,
    sem_surf_send,
    sem_surf,
    sem_point_send,
    sem_point,
):
    z = lax.axis_index("inner")
    me = lax.axis_index("outer")
    blocks, rc = energy_hbm.shape
    rows = 2 * blocks
    nc, nr = grid.shape[2] - 2 * ch, grid.shape[3]
    ext = edge_out.shape[2]
    depth = 2 * blocks * rc
    near = rows - 2
    has_below = z > 0
    has_above = z < planes - 1
    power = sectors & (sectors - 1) == 0

    def partner(s):
        if not power:
            return lax.rem(me + s, sectors)
        to, bit = me, 1
        while bit < sectors:
            if s & bit:
                to = to + bit * (1 - 2 * ((me // bit) % 2))
            bit *= 2
        return to

    def source(s):
        return partner(s) if power else lax.rem(me + sectors - s, sectors)

    def remote(src, dst, send, recv, plane, sector):
        return pltpu.make_async_remote_copy(
            src_ref=src,
            dst_ref=dst,
            send_sem=send,
            recv_sem=recv,
            device_id={"inner": plane, "outer": sector},
            device_id_type=MESH,
        )

    def wait(ref, sem):
        pltpu.make_async_copy(ref, ref, sem).wait()

    barrier = pltpu.get_barrier_semaphore()

    def greet(plane, s):
        pl.semaphore_signal(
            barrier,
            inc=1,
            device_id={"inner": plane, "outer": partner(s)},
            device_id_type=MESH,
        )

    for s in range(sectors - 1, 0, -1):
        greet(z, s)

    @pl.when(has_below)
    def _():
        for s in range(sectors - 1, -1, -1):
            greet(z - 1, s)

    @pl.when(has_above)
    def _():
        for s in range(sectors - 1, -1, -1):
            greet(z + 1, s)

    own = pl.ds(ch, nc)
    small_loads = [
        pltpu.make_async_copy(src, dst, sem_small.at[i])
        for i, (src, dst) in enumerate(
            (
                (inner_hbm, inner_ref),
                (size_hbm, size_ref),
                (coef_hbm, coef_ref),
                (pattern_hbm, pattern_ref),
                (surface_hbm, surface_ref),
                (threshold_hbm, threshold_ref),
                (energy_hbm, energy_ref),
                (field_hbm, field_ref),
            )
        )
    ]
    for load in small_loads:
        load.start()
    states = []
    for p in range(2):
        states.append(
            pltpu.make_async_copy(outer_hbm.at[p], grid.at[0, p, own, :], sem_outer.at[p])
        )
        states.append(
            pltpu.make_async_copy(
                outer_hbm.at[p, pl.ds(nc - ch, ch)], halo_out.at[p, 0], sem_outer.at[2 + p]
            )
        )
        states.append(
            pltpu.make_async_copy(
                outer_hbm.at[p, pl.ds(0, ch)], halo_out.at[p, 1], sem_outer.at[4 + p]
            )
        )
        states.append(
            pltpu.make_async_copy(outer_hbm.at[p], outer_out.at[p], sem_outer.at[6 + p])
        )
    for p in (1, 0):
        states[4 * p + 1].start()
        states[4 * p + 2].start()
    loads = [
        pltpu.make_async_copy(
            dipole_hbm.at[pl.ds(l * rc, rc)], dip_full.at[pl.ds(l * rc, rc)], sem_load.at[l]
        )
        for l in range(blocks)
    ]
    for load in loads:
        load.start()
    for p in range(2):
        states[4 * p].start()
        states[4 * p + 3].start()

    raw_rows[...] = jnp.zeros_like(raw_rows)

    @pl.when(z == 0)
    def _():
        below_in[...] = jnp.zeros_like(below_in)
        grid[:, :, 0:ch, :] = jnp.zeros((2, 2, ch, nr), f32)

    @pl.when(z == planes - 1)
    def _():
        above_in[...] = jnp.zeros_like(above_in)
        grid[:, :, ch + nc : 2 * ch + nc, :] = jnp.zeros((2, 2, ch, nr), f32)

    def channel_copies(slot, p):
        up = remote(
            halo_out.at[p, 0],
            grid.at[slot, p, pl.ds(0, ch), :],
            sem_up_send.at[p],
            sem_up_recv.at[slot, p],
            z + 1,
            me,
        )
        down = remote(
            halo_out.at[p, 1],
            grid.at[slot, p, pl.ds(ch + nc, ch), :],
            sem_down_send.at[p],
            sem_down_recv.at[slot, p],
            z - 1,
            me,
        )
        return up, down

    for load in small_loads:
        load.wait()

    side = pairs.shape[1]
    for l in range(blocks + 1):
        pairs[l, ch:side, :] = jnp.zeros((side - ch, side), f32)
    for l in range(blocks):
        pairs[l + 1, 0:ch, :] = jnp.zeros((ch, side), f32)
        pairs[l + 1, 0:ch, 0:ch] = coef_ref[l] * pattern_ref[l].astype(f32)

    @pl.when(z == 0)
    def _():
        pairs[0, 0:ch, :] = jnp.zeros((ch, side), f32)

    share = remote(
        pairs.at[blocks, pl.ds(0, ch), :],
        pairs.at[0, pl.ds(0, ch), :],
        sem_g_send,
        sem_g_recv,
        z + 1,
        me,
    )

    order_of = [(l, p) for l in range(blocks) for p in range(2)]
    position = me * rc + lax.broadcasted_iota(jnp.int32, (1, rc), 1)
    live_ref[...] = jnp.concatenate(
        [jnp.where(position < size_ref[:, l : l + 1], 1.0, 0.0) for l, p in order_of], axis=0
    )
    energy_rows[...] = jnp.concatenate([energy_ref[l : l + 1, :] for l, p in order_of], axis=0)
    term[...] = live_ref[...] * jnp.concatenate(
        [inner_ref[p, l : l + 1, :] for l, p in order_of], axis=0
    )
    total_inner[...] = term[...]

    small = lax.broadcasted_iota(jnp.int32, (nc, nc), 0) == lax.broadcasted_iota(
        jnp.int32, (nc, nc), 1
    )
    diag_ref[...] = 2.0 * kinetic_scale + jnp.sum(
        jnp.where(small, threshold_ref[...], 0.0), axis=1, keepdims=True
    )

    surface_ext = jnp.concatenate(
        [
            jnp.zeros((ch, rc), f32),
            surface_ref[...],
            jnp.zeros((ext - ch - nc, rc), f32),
        ],
        axis=0,
    )
    sh, sl = split(surface_ext)
    surf_cat[0:ext, :] = sh
    surf_cat[ext : 2 * ext, :] = sl
    surf_turn[0:rc, :] = sh.T
    surf_turn[rc : 2 * rc, :] = sl.T

    waits = (sectors - 1) + sectors * (
        jnp.where(has_below, 1, 0) + jnp.where(has_above, 1, 0)
    )
    pl.semaphore_wait(barrier, waits)

    @pl.when(has_above)
    def _():
        share.start()

    for p in (1, 0):
        states[4 * p + 1].wait()
        states[4 * p + 2].wait()
        up, down = channel_copies(0, p)

        @pl.when(has_above)
        def _():
            up.start()

        @pl.when(has_below)
        def _():
            down.start()

    count = STEPS * ORDER
    row_block = lax.broadcasted_iota(jnp.int32, (rows, 1), 0) // 2
    low_lane = ch + ch * (lax.broadcasted_iota(jnp.int32, (rows, ext), 0) // 2)
    lane_of = lax.broadcasted_iota(jnp.int32, (rows, ext), 1)
    own_lanes = (lane_of >= low_lane) & (lane_of < low_lane + ch)

    def eye(count, shift):
        return (
            lax.broadcasted_iota(jnp.int32, (count, ext), 0) + shift
            == lax.broadcasted_iota(jnp.int32, (count, ext), 1)
        )

    def to_row(col):
        return jnp.sum(jnp.where(eye(nc, ch), col, 0.0), axis=0, keepdims=True)

    def to_col(row, count, shift):
        return jnp.sum(jnp.where(eye(count, shift), row, 0.0), axis=1, keepdims=True)

    def spread(v, first, count):
        high, low = halves(v)
        zero = jnp.zeros_like(v)
        top, bottom = [], []
        for l in range(first, first + count):
            mine = row_block == l
            h = jnp.where(mine, high, 0.0)
            top += [h, h]
            bottom += [jnp.where(mine, low, 0.0), zero]
        return jnp.concatenate(
            [jnp.concatenate(top, axis=1), jnp.concatenate(bottom, axis=1)], axis=0
        ).astype(bf16)

    def stacked(v):
        high, low = halves(v)
        return jnp.concatenate(
            [
                jnp.concatenate([high, high], axis=1),
                jnp.concatenate([low, jnp.zeros_like(low)], axis=1),
            ],
            axis=0,
        ).astype(bf16)

    def fold(r):
        return r[:rows] + r[rows:]

    def edge_sends(st, f):
        def three(cond, src, dst, sem, send, sector):
            @pl.when(cond)
            def _():
                f(remote(src, dst(0), send.at[0], sem.at[st, 0], z, sector))

                @pl.when(has_below)
                def _():
                    f(remote(src, dst(2), send.at[1], sem.at[st, 2], z - 1, sector))

                @pl.when(has_above)
                def _():
                    f(remote(src, dst(1), send.at[2], sem.at[st, 1], z + 1, sector))

        three(
            me > 0,
            edge_out.at[st, pl.ds(0, 2)],
            lambda o: right_in.at[st, o, pl.ds(0, 2)],
            sem_right,
            sem_e_send.at[0],
            me - 1,
        )
        three(
            me < sectors - 1,
            edge_out.at[st + SLOTS, pl.ds(0, 2)],
            lambda o: left_in.at[st, o, pl.ds(0, 2)],
            sem_left,
            sem_e_send.at[1],
            me + 1,
        )

    def surf_sends(st, f):
        src = surf_in.at[st, 0, me, pl.ds(0, 2)]

        @pl.when(me > 0)
        def _():
            f(remote(src, src, sem_surf_send.at[0], sem_surf.at[st, 0], z, 0))

        @pl.when(has_below)
        def _():
            dst = surf_in.at[st, 2, me, pl.ds(0, 2)]
            f(remote(src, dst, sem_surf_send.at[1], sem_surf.at[st, 2], z - 1, 0))

        @pl.when(has_above)
        def _():
            dst = surf_in.at[st, 1, me, pl.ds(0, 2)]
            f(remote(src, dst, sem_surf_send.at[2], sem_surf.at[st, 1], z + 1, 0))

    def point_sends(st, f):
        @pl.when(me == 0)
        def _():
            src = point_in.at[st, pl.ds(0, 2)]
            for k in range(1, sectors):
                f(remote(src, src, sem_point_send.at[k], sem_point.at[st], z, k))

    def edge_wait(sl, o):
        @pl.when(me > 0)
        def _():
            wait(left_in.at[sl, o, pl.ds(0, 2)], sem_left.at[sl, o])

        @pl.when(me < sectors - 1)
        def _():
            wait(right_in.at[sl, o, pl.ds(0, 2)], sem_right.at[sl, o])

        @pl.when(me == 0)
        def _():
            first = 1 if o == 0 else 0
            wait(
                surf_in.at[sl, o, pl.ds(first, sectors - first), pl.ds(0, 2)],
                sem_surf.at[sl, o],
            )

    def edge_waits_beyond(sl):
        @pl.when(has_below)
        def _():
            edge_wait(sl, 1)

        @pl.when(has_above)
        def _():
            edge_wait(sl, 2)

    def edge_rows(sl, o):
        total_b = surf_in[sl, o, 0]
        for k in range(1, sectors):
            total_b = total_b + surf_in[sl, o, k]
        left = jnp.where(me == 0, total_b, left_in[sl, o])
        right = jnp.where(me == sectors - 1, 0.0, right_in[sl, o])
        if o == 1:
            left, right = jnp.where(has_below, left, 0.0), jnp.where(has_below, right, 0.0)
        if o == 2:
            left, right = jnp.where(has_above, left, 0.0), jnp.where(has_above, right, 0.0)
        return left, right

    lane = lax.broadcasted_iota(jnp.int32, (1, 128), 1)

    def scales(t):
        order = lax.rem(t, ORDER)
        factor = time_step / (order + 1).astype(f32)
        return factor * kinetic_scale, -factor * kinetic_scale

    def correct_own(t, par, refresh):
        valid = t >= 0
        sl = lax.rem(t + SLOTS, SLOTS)
        t = jnp.maximum(t, 0)
        left, right = [jnp.where(valid, row, 0.0) for row in edge_rows(sl, 0)]
        for d, scale in ((1, scales(t)[0]), (0, scales(t)[1])):
            first = jnp.where(lane == 0, scale * to_col(left[1 - d : 2 - d], nc, ch), 0.0)
            last = jnp.where(lane == 127, scale * to_col(right[1 - d : 2 - d], nc, ch), 0.0)
            outer_out[d, :, 0:128] += first
            outer_out[d, :, nr - 128 : nr] += last
            if refresh:
                grid[par, d, own, 0:128] += first
                grid[par, d, own, nr - 128 : nr] += last

    def a_copies(par):
        here = peer_in.at[par, me, pl.ds(0, near)]
        return [
            remote(here, here, sem_a_send.at[s], sem_a_recv.at[par, s], z, partner(s))
            for s in range(sectors - 1, 0, -1)
        ]

    def z_copies(par):
        return [
            remote(
                first_out.at[par, pl.ds(0, 2)],
                above_in.at[par, me, pl.ds(0, 2)],
                sem_z_send.at[s],
                sem_z_recv.at[par, s],
                z - 1,
                partner(s),
            )
            for s in range(sectors - 1, -1, -1)
        ]

    def b_copy(par, s):
        return remote(
            part_out.at[s, pl.ds(0, near)],
            part_in.at[par, me, pl.ds(0, near)],
            sem_b_send.at[s],
            sem_b_recv.at[par, s],
            z,
            partner(s),
        )

    def y_copy(par, s):
        return remote(
            far_out.at[s, pl.ds(0, 2)],
            below_in.at[par, me, pl.ds(0, 2)],
            sem_y_send.at[s],
            sem_y_recv.at[par, s],
            z + 1,
            partner(s),
        )

    def send_state(t):
        par = lax.rem(t, 2)
        c = term[...]
        first_out[par] = c
        peer_in[par, me] = pltpu.roll(c, rows - 2, 0)

        @pl.when(has_below)
        def _():
            for copy in z_copies(par):
                copy.start()

        for copy in a_copies(par):
            copy.start()

    row_of = lax.broadcasted_iota(jnp.int32, (8, 1), 0)

    def send_edges(t):
        st = lax.rem(t, SLOTS)
        edge_out[st] = raw_rows[0]
        edge_out[st + SLOTS] = raw_rows[1]

        @pl.when(t > 0)
        def _():
            sl = lax.rem(t + SLOTS - 1, SLOTS)
            edge_wait(sl, 0)
            one, zero = scales(t - 1)
            scale = jnp.where(row_of == 0, zero, one)
            for e, row in enumerate(edge_rows(sl, 0)):
                row = jnp.where(row_of == 0, pltpu.roll(row, 7, 0), pltpu.roll(row, 1, 0))
                edge_out[st + e * SLOTS] += scale * row

        @pl.when(me == 0)
        def _():
            point_in[st] = edge_out[st]

        point_sends(st, lambda copy: copy.start())
        edge_sends(st, lambda copy: copy.start())

    def send_back(t):
        par = lax.rem(t, 2)
        st = lax.rem(t, SLOTS)
        c = term[...]
        lhs = stacked(c)

        def product(l, s):
            at = pl.ds(pl.multiple_of(partner(s) * rc, 128), rc)
            return fold(dot(lhs, dip_cat[2 * l * rc : 2 * (l + 1) * rc, at]))

        def group(chosen):
            for s in chosen:
                far_out[s] = pltpu.roll(product(blocks - 1, s), 2, 0)
                back = jnp.zeros((rows, rc), f32)
                for l in range(blocks - 1):
                    back = jnp.where(row_block == l, product(l, s), back)
                if s:
                    part_out[s] = back
                else:
                    part_in[par, me] = back

            @pl.when(has_above)
            def _():
                for s in chosen:
                    y_copy(par, s).start()

            for s in chosen:
                if s:
                    b_copy(par, s).start()

        def send_surf():
            b = fold(dot(lhs, surf_turn[...]))
            b = jnp.where(own_lanes, b, 0.0)
            total_b = b
            for l in range(1, blocks):
                total_b = total_b + pltpu.roll(b, 2 * l, 0)
            surf_in[st, 0, me] = total_b
            surf_sends(st, lambda copy: copy.start())

        order = list(range(sectors - 1, -1, -1))
        group(order[: sectors // 2])
        send_surf()
        send_edges(t)
        group(order[sectors // 2 :])

    send_state(jnp.int32(0))
    for l in range(blocks):
        loads[l].wait()

        def divide(k, carry):
            at = pl.ds(pl.multiple_of(k * rc, 128), rc)
            high, low = split(dip_full[l * rc : (l + 1) * rc, at])
            dip_cat[2 * l * rc : (2 * l + 1) * rc, at] = high
            dip_cat[(2 * l + 1) * rc : (2 * l + 2) * rc, at] = low
            return carry

        lax.fori_loop(0, sectors, divide, 0, unroll=2)

    for p in range(2):
        states[4 * p].wait()
        states[4 * p + 3].wait()
        raw_rows[0, p : p + 1, :] = to_row(grid[0, p, own, 0:1])
        raw_rows[1, p : p + 1, :] = to_row(grid[0, p, own, nr - 1 : nr])
    send_back(jnp.int32(0))
    for l in range(blocks):

        def turn(k, carry):
            at = pl.ds(pl.multiple_of(k * rc, 128), rc)
            base = k * depth + 2 * l * rc
            high = dip_cat[2 * l * rc : (2 * l + 1) * rc, at]
            low = dip_cat[(2 * l + 1) * rc : (2 * l + 2) * rc, at]
            dip_turn[pl.ds(pl.multiple_of(base, 128), rc), :] = high.T
            dip_turn[pl.ds(pl.multiple_of(base + rc, 128), rc), :] = low.T
            return carry

        lax.fori_loop(0, sectors, turn, 0, unroll=2)

    @pl.when(has_below)
    def _():
        share.wait_recv()

    @pl.when(has_above)
    def _():
        share.wait_send()

    reach = -(-(nc + 2 * ch) // 128) * 128
    fill = jnp.zeros((ch, reach - side), f32)
    mixed_rows = []
    for l in range(blocks):
        upward = jnp.concatenate([pairs[l + 1, 0:ch, :], fill], axis=1)
        downward = jnp.concatenate([pairs[l].T[0:ch], fill], axis=1)
        upward = pltpu.roll(upward, (l + 2) * ch, 1)
        if l:
            downward = pltpu.roll(downward, l * ch, 1)
        mixed_rows.append((upward + downward)[:, 0 : nc + 2 * ch])
    mh, ml = split(jnp.concatenate(mixed_rows, axis=0))
    mix_split[0:nc, :] = mh
    mix_split[nc : 2 * nc, :] = ml

    def apply(t, carry):
        par = lax.rem(t, 2)
        nxt = 1 - par
        st = lax.rem(t, SLOTS)
        order = lax.rem(t, ORDER)
        step = lax.div(t, ORDER)
        strength = field_ref[:, 0:1]
        for i in range(1, STEPS):
            strength = jnp.where(step == i, field_ref[:, i : i + 1], strength)
        factor = time_step / (order + 1).astype(f32)
        last = order == ORDER - 1

        @pl.when(t > 0)
        def _():
            edge_waits_beyond(lax.rem(t + SLOTS - 1, SLOTS))

        def unit_wait(q):
            p = lax.rem(t + 1 + q, 2)
            up, down = channel_copies(par, p)
            up_old, down_old = channel_copies(par, 1 - p)

            @pl.when(has_below)
            def _():
                up.wait_recv()
                down_old.wait_send()

            @pl.when(has_above)
            def _():
                down.wait_recv()
                up_old.wait_send()

        def unit_start(q):
            p = lax.rem(t + 1 + q, 2)
            imag = p == 1
            past = jnp.maximum(t - 1, 0)
            sl = lax.rem(t + SLOTS - 1, SLOTS)
            one, zero = scales(past)
            scale = jnp.where(imag, one, zero)
            for o, start, shift in ((1, 0, nc), (2, ch + nc, ch)):
                left, right = [jnp.where(t > 0, row, 0.0) for row in edge_rows(sl, o)]
                left = jnp.where(imag, left[0:1], left[1:2])
                right = jnp.where(imag, right[0:1], right[1:2])
                at = pl.ds(start, ch)
                grid[par, p, at, 0:128] += jnp.where(
                    lane == 0, scale * to_col(left, ch, shift), 0.0
                )
                grid[par, p, at, nr - 128 : nr] += jnp.where(
                    lane == 127, scale * to_col(right, ch, shift), 0.0
                )
            gh, gl = split(grid[par, p])
            r = dot(mix_split[...], gh)
            return r[:nc] + r[nc:] + dot(mix_split[0:nc, :], gl)

        def unit_finish(q, coupled):
            p = lax.rem(t + 1 + q, 2)
            imag = p == 1
            x = grid[par, p, own, :]
            lanes = lax.broadcasted_iota(jnp.int32, (1, nr), 1)
            left = jnp.where(lanes == 0, 0.0, pltpu.roll(x, 1, 1))
            right = jnp.where(lanes == nr - 1, 0.0, pltpu.roll(x, nr - 1, 1))
            image = diag_ref[...] * x - kinetic_scale * (left + right) + strength * coupled
            value = jnp.where(imag, factor, -factor) * image
            acc = outer_out[1 - p] + value
            outer_out[1 - p] = acc
            value = jnp.where(last, acc, value)
            grid[nxt, 1 - p, own, :] = value
            raw_rows[0, pl.ds(1 - p, 1), :] = to_row(value[:, 0:1])
            raw_rows[1, pl.ds(1 - p, 1), :] = to_row(value[:, nr - 1 : nr])
            halo_out[1 - p, 0] = value[nc - ch : nc]
            halo_out[1 - p, 1] = value[0:ch]

        def unit_send(q):
            p = lax.rem(t + 1 + q, 2)
            up_new, down_new = channel_copies(nxt, 1 - p)

            @pl.when(jnp.logical_and(has_above, t < STEPS * ORDER - 1))
            def _():
                up_new.start()

            @pl.when(jnp.logical_and(has_below, t < STEPS * ORDER - 1))
            def _():
                down_new.start()

        def take_wait(group):
            for s in group:
                if s:
                    wait(peer_in.at[par, source(s), pl.ds(0, near)], sem_a_recv.at[par, s])

        def take(groups, first, count):
            total = jnp.zeros((rows, rc), f32)
            for group in (groups[0::2], groups[1::2]):
                sums = [None] * count
                for s in group:
                    k = source(s)
                    if first:
                        left = stacked(pltpu.roll(above_in[par, k], rows - 2, 0))
                    else:
                        left = stacked(peer_in[par, k])
                    for i in range(count):
                        base = k * depth + 2 * (first + i) * rc
                        at = pl.ds(pl.multiple_of(base, 128), 2 * rc)
                        part = dot(left, dip_turn[at, :])
                        sums[i] = part if sums[i] is None else sums[i] + part
                for i in range(count):
                    total = total + jnp.where(row_block == first + i, fold(sums[i]), 0.0)
            return total

        middle = list(range(2, sectors * 3 // 4))
        tail = list(range(sectors * 3 // 4, sectors))

        unit_wait(0)
        take_wait([0, 1])
        correct_own(t - 1, par, True)
        coupled = unit_start(0)
        ahead = take([0, 1], 0, blocks - 1)
        unit_finish(0, coupled)
        unit_send(0)

        unit_wait(1)
        take_wait(middle)
        coupled = unit_start(1)
        ahead = ahead + take(middle, 0, blocks - 1)
        unit_finish(1, coupled)
        unit_send(1)

        take_wait(tail)

        @pl.when(me > 0)
        def _():
            wait(point_in.at[st, pl.ds(0, 2)], sem_point.at[st])

        def far_wait(group):
            @pl.when(has_above)
            def _():
                for s in group:
                    wait(above_in.at[par, source(s), pl.ds(0, 2)], sem_z_recv.at[par, s])

        far_wait([0, 1] + middle)
        ahead = ahead + take(tail, 0, blocks - 1)
        point = jnp.concatenate([point_in[st, 0:2]] * blocks, axis=0)
        surf = fold(dot(stacked(jnp.where(own_lanes, point, 0.0)), surf_cat[...]))
        ahead = ahead + take([0, 1] + middle, blocks - 1, 1)

        for s in range(1, sectors):
            wait(part_in.at[par, source(s), pl.ds(0, near)], sem_b_recv.at[par, s])
        far_wait(tail)

        @pl.when(has_below)
        def _():
            for s in range(sectors):
                wait(below_in.at[par, source(s), pl.ds(0, 2)], sem_y_recv.at[par, s])

        ahead = ahead + take(tail, blocks - 1, 1)
        behind = part_in[par, 0]
        for k in range(1, sectors):
            behind = behind + part_in[par, k]
        far = below_in[par, 0]
        for k in range(1, sectors):
            far = far + below_in[par, k]
        behind = jnp.where(row_block == 0, far, pltpu.roll(behind, 2, 0))
        c = term[...]
        image = live_ref[...] * (
            energy_rows[...] * c + strength * (ahead + behind) - kinetic_scale * surf
        )
        even = lax.rem(lax.broadcasted_iota(jnp.int32, (rows, 1), 0), 2) == 0
        value = factor * jnp.where(
            even, pltpu.roll(image, rows - 1, 0), -pltpu.roll(image, 1, 0)
        )
        acc = total_inner[...] + value
        total_inner[...] = acc
        term[...] = jnp.where(last, acc, value)

        for copy in a_copies(par) + [b_copy(par, s) for s in range(1, sectors)]:
            copy.wait_send()

        @pl.when(has_below)
        def _():
            for copy in z_copies(par):
                copy.wait_send()

        @pl.when(has_above)
        def _():
            for s in range(sectors):
                y_copy(par, s).wait_send()

        surf_sends(st, lambda copy: copy.wait_send())
        point_sends(st, lambda copy: copy.wait_send())
        edge_sends(st, lambda copy: copy.wait_send())

        @pl.when(t < count - 1)
        def _():
            send_state(t + 1)
            send_back(t + 1)

        return carry

    lax.fori_loop(0, count, apply, 0)
    edge_wait((count - 1) % SLOTS, 0)
    edge_waits_beyond((count - 1) % SLOTS)
    correct_own(jnp.int32(count - 1), 0, False)
    final = total_inner[...]
    for p in range(2):
        inner_out[p] = jnp.concatenate(
            [final[2 * l + p : 2 * l + p + 1] for l in range(blocks)], axis=0
        )


def publish(inner_ref, outer_ref, inner_out, outer_out, sem):
    copies = [
        pltpu.make_async_copy(inner_ref, inner_out, sem.at[0]),
        pltpu.make_async_copy(outer_ref, outer_out, sem.at[1]),
    ]
    for copy in copies:
        copy.start()
    for copy in copies:
        copy.wait()


def local(
    planes,
    sectors,
    inner_state,
    outer_state,
    energies,
    dipole,
    surface,
    thresholds,
    coupling_coef,
    coupling_pattern,
    block_sizes,
    field_strength,
):
    blocks, rc, total = dipole.shape
    ch = coupling_coef.shape[1]
    nc, nr = outer_state.shape[1:]
    rows = 2 * blocks
    ext = -(-(nc + 2 * ch) // 128) * 128
    vmem = pl.BlockSpec(memory_space=pltpu.VMEM)
    hbm = pl.BlockSpec(memory_space=pltpu.HBM)
    dma = pltpu.SemaphoreType.DMA
    side = -(-ch // 128) * 128
    inner, outer = pl.pallas_call(
        functools.partial(kernel, planes, sectors, ch),
        out_shape=(
            jax.ShapeDtypeStruct((2, blocks, rc), f32),
            jax.ShapeDtypeStruct((2, nc, nr), f32),
        ),
        in_specs=[hbm] * 10,
        out_specs=(vmem, vmem),
        scratch_shapes=[
            pltpu.VMEM((2, blocks, rc), f32),
            pltpu.VMEM((blocks, rc), f32),
            pltpu.VMEM((nc, rc), f32),
            pltpu.VMEM((1, nc), f32),
            pltpu.VMEM((blocks, ch, ch), f32),
            pltpu.VMEM((blocks, ch, ch), jnp.int32),
            pltpu.VMEM((1, blocks), jnp.int32),
            pltpu.VMEM((1, STEPS), f32),
            dma((8,)),
            pltpu.VMEM((blocks * rc, total), f32),
            pltpu.VMEM((2 * blocks * rc, total), bf16),
            pltpu.VMEM((2 * blocks * total, rc), bf16),
            pltpu.VMEM((2 * ext, rc), bf16),
            pltpu.VMEM((2 * rc, ext), bf16),
            pltpu.VMEM((2 * nc, nc + 2 * ch), bf16),
            pltpu.VMEM((2, 2, nc + 2 * ch, nr), f32),
            pltpu.VMEM((2, 2, ch, nr), f32),
            pltpu.VMEM((rows, rc), f32),
            pltpu.VMEM((2, sectors, rows, rc), f32),
            pltpu.VMEM((2, rows, rc), f32),
            pltpu.VMEM((2, sectors, rows, rc), f32),
            pltpu.VMEM((sectors, rows, rc), f32),
            pltpu.VMEM((2, sectors, rows, rc), f32),
            pltpu.VMEM((sectors, rows, rc), f32),
            pltpu.VMEM((2, sectors, rows, rc), f32),
            pltpu.VMEM((blocks + 1, side, side), f32),
            pltpu.VMEM((rows, rc), f32),
            pltpu.VMEM((rows, rc), f32),
            pltpu.VMEM((rows, rc), f32),
            pltpu.VMEM((nc, 1), f32),
            pltpu.VMEM((2, 8, ext), f32),
            pltpu.VMEM((2 * SLOTS, 8, ext), f32),
            pltpu.VMEM((SLOTS, 3, 8, ext), f32),
            pltpu.VMEM((SLOTS, 3, 8, ext), f32),
            pltpu.VMEM((SLOTS, 3, sectors, 8, ext), f32),
            pltpu.VMEM((SLOTS, 8, ext), f32),
            dma((blocks,)), dma((8,)), dma(()), dma(()),
            dma((sectors,)), dma((2, sectors)),
            dma((sectors,)), dma((2, sectors)),
            dma((sectors,)), dma((2, sectors)),
            dma((sectors,)), dma((2, sectors)),
            dma((2,)), dma((2, 2)), dma((2,)), dma((2, 2)),
            dma((2, 3)), dma((SLOTS, 3)), dma((SLOTS, 3)),
            dma((3,)), dma((SLOTS, 3)),
            dma((sectors,)), dma((SLOTS,)),
        ],
        compiler_params=pltpu.CompilerParams(
            collective_id=0, has_side_effects=True, vmem_limit_bytes=56 * 1024 * 1024
        ),
    )(
        inner_state,
        outer_state,
        energies,
        dipole.reshape(blocks * rc, total),
        surface.reshape(nc, rc),
        thresholds.reshape(1, nc),
        coupling_coef,
        coupling_pattern,
        block_sizes.reshape(1, blocks),
        field_strength.reshape(1, STEPS),
    )
    return pl.pallas_call(
        publish,
        out_shape=(
            jax.ShapeDtypeStruct((2, blocks, rc), f32),
            jax.ShapeDtypeStruct((2, nc, nr), f32),
        ),
        in_specs=[vmem] * 2,
        out_specs=(hbm, hbm),
        scratch_shapes=[dma((2,))],
    )(inner, outer)


def solution(mesh):
    placed = (
        P(None, "inner", "outer"),
        P(None, "inner", "outer"),
        P("inner", "outer"),
        P("inner", "outer", None),
        P("inner", None, "outer"),
        P("inner"),
        P("inner", None, None),
        P("inner", None, None),
        P("inner"),
        P(),
    )
    return jax.shard_map(
        functools.partial(local, mesh.shape["inner"], mesh.shape["outer"]),
        mesh=mesh,
        in_specs=placed,
        out_specs=(P(None, "inner", "outer"), P(None, "inner", "outer")),
        check_vma=False,
    )
```

time: 61.9 us -> 58.3 us (0.942)
  local copies, waits for them, and re-layouts: 3.26 us -> 0 us
    unnamed x2 -> x0, local copies, waits for them, and re-layouts: 3.26 us -> none
    pallas_call x1, Pallas kernels: 57.7 us -> 55.5 us  [local(): pl.pallas_call(functools.partial(kernel, planes, sectors, ch), out_shape=...]
    pallas_call x0 -> x1, Pallas kernels: none -> 1.96 us  [local(): pl.pallas_call(publish, out_shape=(jax.ShapeDtypeStruct((2, blocks, rc),...]
where the time goes in v2:
time: 58.3 us; the launch traced here: 58.1 us
  Pallas kernels  57.5 us (99%)
  between operations  0.64 us (1%)
    pallas_call x1, Pallas kernels, local(): pl.pallas_call(functools.partial(kernel, planes, sectors, ch), out_shape=...  55.5 us
    pallas_call x1, Pallas kernels, local(): pl.pallas_call(publish, out_shape=(jax.ShapeDtypeStruct((2, blocks, rc),...  1.96 us

profile of v2, /device:TPU:0, one launch (start us, length us, event | category | flops | bytes accessed | tf_op | source)
XLA Modules:
  0.0 58.1 jit_solution(11658770940359157507)
XLA Ops:
  0.6 55.5 %shard_map.113 = (f32[2,4,256]{2,1,0:T(4,128)}, f32[2,160,512]{2,1,0:T(8,128)}) custom-call(f32[2,4,256]{2,1,0:T(4,128)} %inner_hbm.1, f32[2,160,512]{2,1,0:T(8,128)} %outer_hbm.1, f32[4,256]{1,0:T(4,128)} %energy_hbm.1, f32[1024,2048]{1,0:T(8,128)} %bitcast.5, f32[160,256]{1,0:T(8,128)} %bitcast.6, f32[1,160]{1,0:T(1,128)} %bitcast.7, ...), custom_call_target="tpu_custom_call" | custom-call | tf_op jit(solution)/shard_map/pallas_call | solution.py:909
  56.1 2.0 %shard_map.114 = (f32[2,4,256]{2,1,0:T(4,128)}, f32[2,160,512]{2,1,0:T(8,128)}) custom-call(f32[2,4,256]{2,1,0:T(4,128)} %get-tuple-element.4.inner_ref, f32[2,160,512]{2,1,0:T(8,128)} %get-tuple-element.5.outer_ref), custom_call_target="tpu_custom_call" | custom-call | tf_op jit(solution)/shard_map/pallas_call | solution.py:979

commit v3 on v2

--- a/solution.py
+++ b/solution.py
@@ -641,7 +641,7 @@
             dip_turn[pl.ds(pl.multiple_of(base + rc, 128), rc), :] = low.T
             return carry
 
-        lax.fori_loop(0, sectors, turn, 0, unroll=2)
+        lax.fori_loop(0, sectors, turn, 0, unroll=4)
 
     @pl.when(has_below)
     def _():
@@ -872,15 +872,22 @@
         )
 
 
-def publish(inner_ref, outer_ref, inner_out, outer_out, sem):
-    copies = [
-        pltpu.make_async_copy(inner_ref, inner_out, sem.at[0]),
-        pltpu.make_async_copy(outer_ref, outer_out, sem.at[1]),
-    ]
-    for copy in copies:
-        copy.start()
-    for copy in copies:
-        copy.wait()
+def publish(inner_ref, outer_ref, inner_out, outer_out, inner_held, outer_held, sems):
+    count = outer_held.shape[0] * 2
+    nc = outer_held.shape[1] // 2
+    pieces = [(inner_ref, inner_held, inner_out)]
+    for i in range(count):
+        at = (i // 2, pl.ds((i % 2) * nc, nc))
+        pieces.append((outer_ref.at[at], outer_held.at[at], outer_out.at[at]))
+    takes = [pltpu.make_async_copy(a, b, sems.at[0, i]) for i, (a, b, _) in enumerate(pieces)]
+    gives = [pltpu.make_async_copy(b, c, sems.at[1, i]) for i, (_, b, c) in enumerate(pieces)]
+    for take in takes:
+        take.start()
+    for take, give in zip(takes, gives):
+        take.wait()
+        give.start()
+    for give in gives:
+        give.wait()
 
 
 def local(
@@ -982,9 +989,13 @@
             jax.ShapeDtypeStruct((2, blocks, rc), f32),
             jax.ShapeDtypeStruct((2, nc, nr), f32),
         ),
-        in_specs=[vmem] * 2,
+        in_specs=[hbm] * 2,
         out_specs=(hbm, hbm),
-        scratch_shapes=[dma((2,))],
+        scratch_shapes=[
+            pltpu.VMEM((2, blocks, rc), f32),
+            pltpu.VMEM((2, nc, nr), f32),
+            dma((2, 5)),
+        ],
     )(inner, outer)
 
 

time: 58.3 us -> 57.8 us (level)
  no operation moved by 1% of the time
where the time goes in v3:
time: 57.8 us; the launch traced here: 57.6 us
  Pallas kernels  57 us (99%)
  between operations  0.64 us (1%)
    pallas_call x1, Pallas kernels, local(): pl.pallas_call(functools.partial(kernel, planes, sectors, ch), out_shape=...  55.1 us
    pallas_call x1, Pallas kernels, local(): pl.pallas_call(publish, out_shape=(jax.ShapeDtypeStruct((2, blocks, rc),...  1.92 us

profile of v3, /device:TPU:0, one launch (start us, length us, event | category | flops | bytes accessed | tf_op | source)
XLA Modules:
  0.0 57.6 jit_solution(2401770768799552324)
XLA Ops:
  0.6 55.1 %shard_map.113 = (f32[2,4,256]{2,1,0:T(4,128)}, f32[2,160,512]{2,1,0:T(8,128)}) custom-call(f32[2,4,256]{2,1,0:T(4,128)} %inner_hbm.1, f32[2,160,512]{2,1,0:T(8,128)} %outer_hbm.1, f32[4,256]{1,0:T(4,128)} %energy_hbm.1, f32[1024,2048]{1,0:T(8,128)} %bitcast.5, f32[160,256]{1,0:T(8,128)} %bitcast.6, f32[1,160]{1,0:T(1,128)} %bitcast.7, ...), custom_call_target="tpu_custom_call" | custom-call | tf_op jit(solution)/shard_map/pallas_call | solution.py:916
  55.7 1.9 %shard_map.114 = (f32[2,4,256]{2,1,0:T(4,128)}, f32[2,160,512]{2,1,0:T(8,128)}) custom-call(f32[2,4,256]{2,1,0:T(4,128)} %get-tuple-element.4.inner_ref, f32[2,160,512]{2,1,0:T(8,128)} %get-tuple-element.5.outer_ref), custom_call_target="tpu_custom_call" | custom-call | tf_op jit(solution)/shard_map/pallas_call | solution.py:986
